TPU v7x, 32 devices: a whole 2x2x4 slice. The times are simulated.
32 devices in a mesh: stream: 4 (over z), patch: 8 (over y, x, core).
Axes of the slice: x: 2, y: 2, z: 4, core: 2. Of those that a mesh axis runs over, the one named last changes fastest.
Arguments:
- tokens: bfloat16 [4, 1024, 1536], P('stream', 'patch'), may hold values from -6 to 6
- query_weight: bfloat16 [1536, 768], P('stream'), may hold values from -0.25 to 0.25
- key_weight: bfloat16 [1536, 768], P('stream'), may hold values from -0.25 to 0.25
- value_weight: bfloat16 [1536, 768], P('stream'), may hold values from -0.15625 to 0.15625
- cache_keys: bfloat16 [4, 6144, 768], P('stream', 'patch'), may hold values from -240 to 240, as said below
- cache_values: bfloat16 [4, 6144, 768], P('stream', 'patch'), may hold values from -6 to 6
- lengths: int32 [4, 8], P('stream', 'patch'), may hold values from 1 to 6, as said below
- assign: int32 [4, 256, 1], P('stream', 'patch'), may hold values from 0 to 7; in each aligned block of 32 rows (0 to 31, 32 to 63, ..., all dimensions but the last counted through in order) at most 8 rows name the same one
Outputs:
- attended: bfloat16 [4, 1024, 768], P('stream', 'patch')
- new_keys: bfloat16 [4, 2048, 768], P('stream', 'patch')
- new_values: bfloat16 [4, 2048, 768], P('stream', 'patch')
Inputs may be any that keep to these rules, and one draw needn't show every extreme that they name: `lengths`: each stream's owners hold whole cache blocks of 128 tokens; in every stream exactly two owners hold 6 blocks and every other owner 1 or 2. `assign`: among the 32 groups of one device no owner is named more than 8 times. `cache_keys`: rows past an owner's length are not part of its cache.
All inputs are finite; a program needn't handle non-finite values.
Results may differ from a plain program's by a relative error of at most 0.015.
The roundings to bfloat16 on the way count: a program that leaves them out, or rounds other values in their place, can miss the bound.
Values may be sent and summed in bfloat16 or wider, within the bound.
No kernel may reach another device: no remote copies, remote signals or barrier semaphores. Data moves between devices by JAX's collectives and lax.ppermute only.
A program may use at most 128 MiB of HBM per device.

v0:
```python
import math
import jax
import jax.numpy as jnp
from jax import lax
from jax.sharding import PartitionSpec as P

HEADS = 6
HD = 128
BLOCK = 128
APP = 4
epsilon = 1e-06
masked_score = -1e30


def body(tokens, query_weight, key_weight, value_weight, cache_keys, cache_values, lengths, assign):
    owners = lax.axis_size("patch")
    span_rows = tokens.shape[1]
    width = HEADS * HD
    floats = tokens[0].astype(jnp.float32)
    normed = (
        floats * lax.rsqrt(jnp.mean(floats * floats, axis=-1, keepdims=True) + epsilon)
    ).astype(jnp.bfloat16)
    gathered = lax.all_gather(normed, "stream", axis=0, tiled=True)
    shard_rows = query_weight.shape[0]
    offset = lax.axis_index("stream") * shard_rows
    columns = lax.dynamic_slice_in_dim(gathered, offset, shard_rows, 1)
    joined = jnp.concatenate((query_weight, key_weight, value_weight), axis=1)
    joined_sum = lax.psum_scatter(
        jnp.dot(columns, joined, preferred_element_type=jnp.float32),
        "stream",
        scatter_dimension=0,
        tiled=True,
    )
    query_sum = joined_sum[:, :width]
    key_sum = joined_sum[:, width : 2 * width]
    value_sum = joined_sum[:, 2 * width :]
    queries = query_sum.astype(jnp.bfloat16)
    keys_new = key_sum.astype(jnp.bfloat16)
    values_new = value_sum.astype(jnp.bfloat16)
    group_count = span_rows // APP
    most_slots = max(2, 2 * group_count // owners)
    owner_ids = assign[0, :, 0]
    positions = jnp.arange(group_count, dtype=jnp.int32)
    earlier = positions[None, :] < positions[:, None]
    matches = owner_ids[:, None] == owner_ids[None, :]
    ranks = jnp.sum(jnp.logical_and(matches, earlier).astype(jnp.int32), axis=1)
    targets = owner_ids * most_slots + ranks
    slot_ids = jnp.arange(owners * most_slots, dtype=jnp.int32)
    select = (targets[None, :] == slot_ids[:, None]).astype(jnp.bfloat16)
    grouped = jnp.concatenate(
        (keys_new.reshape(group_count, APP * width), values_new.reshape(group_count, APP * width)),
        axis=1,
    )
    outgoing = jnp.dot(select, grouped, preferred_element_type=jnp.float32).astype(jnp.bfloat16)
    flags_out = jnp.sum(select.astype(jnp.float32), axis=1).astype(jnp.bfloat16)
    incoming, flags_in = (
        lax.all_to_all(outgoing, "patch", split_axis=0, concat_axis=0, tiled=True),
        lax.all_to_all(flags_out, "patch", split_axis=0, concat_axis=0, tiled=True),
    )
    slot_rows = incoming.shape[0] * APP
    app_keys = incoming[:, : APP * width].reshape(slot_rows, width)
    app_values = incoming[:, APP * width :].reshape(slot_rows, width)
    row_valid = jnp.repeat(flags_in, APP) > 0.5
    all_queries = lax.all_gather(queries, "patch", axis=0, tiled=True).reshape(-1, HEADS, HD)
    scale = 1.0 / math.sqrt(HD)
    cache_k = cache_keys[0]
    cache_v = cache_values[0]
    block_count = lengths[0, 0]

    def fold_block(state, key_rows, value_rows, live):
        best, numer_acc, total_acc = state
        scores = (
            jnp.einsum(
                "thd,khd->thk",
                all_queries,
                key_rows.reshape(-1, HEADS, HD),
                preferred_element_type=jnp.float32,
            )
            * scale
        )
        if live is not None:
            scores = jnp.where(live[None, None, :], scores, masked_score)
        block_top = jnp.max(scores, axis=2)
        weights = jnp.exp(scores - block_top[:, :, None])
        if live is not None:
            weights = jnp.where(live[None, None, :], weights, 0.0)
        weights = weights.astype(jnp.bfloat16)
        part_numer = jnp.einsum(
            "thk,khd->thd",
            weights,
            value_rows.reshape(-1, HEADS, HD),
            preferred_element_type=jnp.float32,
        )
        part_total = jnp.sum(weights.astype(jnp.float32), axis=2)
        merged = jnp.maximum(best, block_top)
        old_scale = jnp.exp(best - merged)
        new_scale = jnp.exp(block_top - merged)
        numer_acc = numer_acc * old_scale[:, :, None] + part_numer * new_scale[:, :, None]
        total_acc = total_acc * old_scale + part_total * new_scale
        return (merged, numer_acc, total_acc)

    query_count = all_queries.shape[0]
    start_state = (
        jnp.full((query_count, HEADS), masked_score, jnp.float32),
        jnp.zeros((query_count, HEADS, HD), jnp.float32),
        jnp.zeros((query_count, HEADS), jnp.float32),
    )
    state = fold_block(start_state, app_keys, app_values, row_valid)

    def per_block(block, state):
        key_rows = lax.dynamic_slice_in_dim(cache_k, block * BLOCK, BLOCK, 0)
        value_rows = lax.dynamic_slice_in_dim(cache_v, block * BLOCK, BLOCK, 0)
        return fold_block(state, key_rows, value_rows, None)

    top_row, numer, total = lax.fori_loop(0, block_count, per_block, state)
    got_numer, got_top, got_total = (
        lax.all_to_all(
            numer.reshape(1, -1, width), "patch", split_axis=1, concat_axis=0, tiled=True
        ),
        lax.all_to_all(top_row[None], "patch", split_axis=1, concat_axis=0, tiled=True),
        lax.all_to_all(total[None], "patch", split_axis=1, concat_axis=0, tiled=True),
    )
    best = jnp.max(got_top, axis=0)
    factor = jnp.exp(got_top - best[None])
    sum_numer = jnp.sum(
        got_numer.reshape(owners, span_rows, HEADS, HD) * factor[:, :, :, None], axis=0
    )
    sum_total = jnp.sum(got_total * factor, axis=0)
    result = sum_numer / sum_total[:, :, None]
    attended = result.reshape(1, span_rows, width).astype(jnp.bfloat16)
    return (attended, app_keys[None], app_values[None])


def solution(mesh):
    placed = (
        P("stream", "patch", None),
        P("stream", None),
        P("stream", None),
        P("stream", None),
        P("stream", "patch", None),
        P("stream", "patch", None),
        P("stream", "patch"),
        P("stream", "patch", None),
    )
    return jax.shard_map(
        body,
        mesh=mesh,
        in_specs=placed,
        out_specs=(
            P("stream", "patch", None),
            P("stream", "patch", None),
            P("stream", "patch", None),
        ),
        check_vma=False,
    )
```

profile of v0, /device:TPU:0, one launch (start us, length us, event | category | flops | bytes accessed | tf_op | source)
XLA Modules:
  0.0 303.4 jit_solution(281291631412131650)
XLA Ops:
  8.4 1.9 fusion.17
  10.3 39.8 %all-gather.3.cloned.1.call-done = bf16[512,1536]{1,0:T(8,128)(2,1)} async-done(((bf16[128,1536]{1,0:T(8,128)(2,1)}), bf16[512,1536]{1,0:T(8,128)(2,1)}) %all-gather.3.cloned.1.call-update) | async-done | bytes 1572880 | tf_op jit(solution)/shard_map/all_gather | solution.py:23
  50.2 5.1 %fusion.10 = f32[512,2304]{1,0:T(8,128)} fusion(bf16[384,768]{1,0:T(8,128)(2,1)} %param.13, bf16[384,768]{1,0:T(8,128)(2,1)} %param.12, bf16[384,768]{1,0:T(8,128)(2,1)} %param.11, bf16[512,1536]{1,0:T(8,128)(2,1)} %all-gather.3.cloned.1.call-done, s32[]{:T(128)S(6)} %select_n.17), kind=kOutput, calls=%fused_computation.25 | convolution fusion | flops 911278080 | bytes 6881284 | tf_op jit(solution)/shard_map/dot_general | solution.py:29
  55.3 84.3 %reduce-scatter.2.cloned.1.call-done = f32[128,2304]{1,0:T(8,128)} async-done(((f32[512,2304]{1,0:T(8,128)}), f32[128,2304]{1,0:T(8,128)}) %reduce-scatter.2.cloned.1.call-update) | async-done | bytes 1179664 | tf_op jit(solution)/shard_map/reduce_scatter | solution.py:28
  139.6 1.3 convert.7
  142.6 3.7 %all-to-all-start = ((bf16[8,8,1]{1,2,0:T(2,128)(2,1)}), bf16[8,8,1]{1,2,0:T(2,128)(2,1)S(1)}, u32[]{:S(2)}, u32[]{:S(2)}) async-start(bf16[8,8,1]{1,2,0:T(2,128)(2,1)} %all_to_all.52), calls=%async_computation | async-start | bytes 8192 | tf_op jit(solution)/shard_map/all_to_all | solution.py:58
  146.6 1.4 fusion.5
  147.9 3.0 all-to-all-done
  150.9 3.5 %all-to-all-start.1 = ((bf16[8,8,6144]{2,1,0:T(8,128)(2,1)}), bf16[8,8,6144]{2,1,0:T(8,128)(2,1)S(1)}, u32[]{:S(2)}, u32[]{:S(2)}) async-start(bf16[8,8,6144]{2,1,0:T(8,128)(2,1)} %fusion.5), calls=%async_computation.2 | async-start | bytes 1572864 | tf_op jit(solution)/shard_map/all_to_all | solution.py:57
  154.5 1.5 copy.109
  155.9 1.4 copy.110
  157.7 13.4 %all-to-all-done.1 = bf16[8,8,6144]{2,1,0:T(8,128)(2,1)S(1)} async-done(((bf16[8,8,6144]{2,1,0:T(8,128)(2,1)}), bf16[8,8,6144]{2,1,0:T(8,128)(2,1)S(1)}, u32[]{:S(2)}, u32[]{:S(2)}) %all-to-all-start.1) | async-done | bytes 786464 | tf_op jit(solution)/shard_map/all_to_all | solution.py:57
  171.7 1.3 reshape_reshape.7
  173.0 1.7 copy.104
  174.7 1.6 copy.111
  177.5 2.1 convert_reduce_fusion.1
  181.1 40.9 %while.14 = (s32[]{:T(128)}, f32[1024,6]{0,1:T(8,128)}, f32[1024,6,128]{0,2,1:T(8,128)S(1)}, f32[1024,6]{0,1:T(8,128)}, s32[]{:T(128)}, /*index=5*/bf16[768,768]...) while((s32[]{:T(128)}, f32[1024,6]{0,1:T(8,128)}, ...), condition=%wide.region_9.10_spmd, body=%wide.region_6.9_spmd.sunk | while | flops 412901376 | bytes 19218712 | solution.py:115
  182.8 2.1 bitcast_reduce_fusion.3
  186.1 1.6 fusion.50
  189.5 2.1 bitcast_reduce_fusion.3
  192.8 1.6 fusion.50
  196.2 2.1 bitcast_reduce_fusion.3
  199.5 1.6 fusion.50
  202.9 2.1 bitcast_reduce_fusion.3
  206.2 1.6 fusion.50
  209.5 2.1 bitcast_reduce_fusion.3
  212.9 1.6 fusion.50
  216.2 2.1 bitcast_reduce_fusion.3
  219.5 1.6 fusion.50
  222.0 1.8 copy.113
  224.3 3.8 %reduce.6 = f32[1024,6]{1,0:T(8,128)} reduce(f32[1024,1,6]{2,1,0:T(1,128)} %bitcast.94, f32[]{:T(128)} %broadcast.73), dimensions={1}, to_apply=%bitcast.56.reduce_sub_computation | reduce | bytes 49156
  228.1 2.0 reshape.145
  230.1 3.9 %all-to-all-start.3 = ((f32[8,1,768]{2,1,0:T(1,128)}), f32[8,1,768]{2,1,0:T(1,128)}, u32[]{:S(2)}, u32[]{:S(2)}) async-start(f32[8,1,768]{2,1,0:T(1,128)} %reshape.145), calls=%async_computation.4 | async-start | bytes 49152 | tf_op jit(solution)/shard_map/all_to_all | solution.py:120
  234.1 1.8 copy.117
  235.8 3.8 %reduce.4 = f32[1024,6]{1,0:T(8,128)} reduce(f32[1024,1,6]{2,1,0:T(1,128)} %bitcast.95, f32[]{:T(128)} %broadcast.73), dimensions={1}, to_apply=%bitcast.54.reduce_sub_computation | reduce | bytes 49156
  239.6 2.0 reshape.143
  241.7 4.1 %all-to-all-start.4 = ((f32[8,1,768]{2,1,0:T(1,128)}), f32[8,1,768]{2,1,0:T(1,128)}, u32[]{:S(2)}, u32[]{:S(2)}) async-start(f32[8,1,768]{2,1,0:T(1,128)} %reshape.143), calls=%async_computation.5 | async-start | bytes 49152 | tf_op jit(solution)/shard_map/all_to_all | solution.py:121
  245.8 5.5 %copy.112 = f32[1,1024,768]{2,0,1:T(1,128)} copy(f32[1,1024,768]{1,2,0:T(8,128)S(1)} %bitcast.82) | data formatting | bytes 6291456 | tf_op jit(solution)/shard_map/reshape | solution.py:118
  251.2 4.2 %all-to-all-start.2 = ((f32[1,1024,768]{2,0,1:T(1,128)}), f32[1,1024,768]{2,0,1:T(1,128)S(1)}, u32[]{:S(2)}, u32[]{:S(2)}) async-start(f32[1,1024,768]{2,0,1:T(1,128)} %copy.112), calls=%async_computation.3 | async-start | bytes 6291456 | tf_op jit(solution)/shard_map/all_to_all | solution.py:117
  255.4 2.0 broadcast_in_dim_reshape.6
  258.4 1.4 reduce.7
  259.8 1.7 reshape.146
  263.9 1.5 reduce.5
  265.3 1.7 reshape.144
  268.3 1.9 mul.117
  270.2 3.6 %copy.116 = f32[1,8,128,768]{3,2,1,0:T(8,128)} copy(f32[1,8,128,768]{2,3,1,0:T(8,128)} %bitcast.88) | data formatting | bytes 6291456 | tf_op jit(solution)/shard_map/mul | solution.py:126
  274.8 18.5 %all-to-all-done.2 = f32[1,1024,768]{2,0,1:T(1,128)S(1)} async-done(((f32[1,1024,768]{2,0,1:T(1,128)}), f32[1,1024,768]{2,0,1:T(1,128)S(1)}, u32[]{:S(2)}, u32[]{:S(2)}) %all-to-all-start.2) | async-done | bytes 3145760 | tf_op jit(solution)/shard_map/all_to_all | solution.py:117
  293.5 1.7 copy-done
  (119 shorter events, 28.6 us)
Async XLA Ops:
  7.2 43.0 %all-gather.3.cloned.1.call-start = ((), (), s32[]{:S(2)}) async-start(), calls=%async_computation.6 | async-start | bytes 1966080 | tf_op jit(solution)/shard_map/all_gather | solution.py:23
  10.3 129.3 %reduce-scatter.2.cloned.1.call-start = ((), (), s32[]{:S(2)}) async-start(), calls=%async_computation.7 | async-start | bytes 5898240 | tf_op jit(solution)/shard_map/reduce_scatter | solution.py:28
  55.2 86.4 %copy-start.10 = (s32[1,32,1]{1,2,0:T(1,128)S(1)}, s32[1,32,1]{1,2,0:T(1,128)}, u32[]{:S(2)}) copy-start(s32[1,32,1]{1,2,0:T(1,128)} %param.17) | copy-start | bytes 388
  55.3 99.2 %copy-start.8 = (bf16[1,768,768]{2,1,0:T(8,128)(2,1)S(1)}, bf16[1,768,768]{2,1,0:T(8,128)(2,1)}, u32[]{:S(2)}) copy-start(bf16[1,768,768]{2,1,0:T(8,128)(2,1)} %param.14) | copy-start | bytes 3538948
  55.3 117.7 %all-gather.5.cloned.1.call-start = ((), (), s32[]{:S(2)}) async-start(), calls=%async_computation.8 | async-start | bytes 1769472 | tf_op jit(solution)/shard_map/all_gather | solution.py:64
  141.6 14.3 %copy-start.9 = (bf16[1,768,768]{2,1,0:T(8,128)(2,1)S(1)}, bf16[1,768,768]{2,1,0:T(8,128)(2,1)}, u32[]{:S(2)}) copy-start(bf16[1,768,768]{2,1,0:T(8,128)(2,1)} %param.15) | copy-start | bytes 3538948
  142.6 8.3 %all-to-all-start = ((bf16[8,8,1]{1,2,0:T(2,128)(2,1)}), bf16[8,8,1]{1,2,0:T(2,128)(2,1)S(1)}, u32[]{:S(2)}, u32[]{:S(2)}) async-start(bf16[8,8,1]{1,2,0:T(2,128)(2,1)} %all_to_all.52), calls=%async_computation | async-start | bytes 8192 | tf_op jit(solution)/shard_map/all_to_all | solution.py:58
  150.9 20.2 %all-to-all-start.1 = ((bf16[8,8,6144]{2,1,0:T(8,128)(2,1)}), bf16[8,8,6144]{2,1,0:T(8,128)(2,1)S(1)}, u32[]{:S(2)}, u32[]{:S(2)}) async-start(bf16[8,8,6144]{2,1,0:T(8,128)(2,1)} %fusion.5), calls=%async_computation.2 | async-start | bytes 1572864 | tf_op jit(solution)/shard_map/all_to_all | solution.py:57
  171.2 1.8 copy-start.1
  177.5 2.7 copy-start.2
  182.8 2.7 copy-start.3
  182.8 2.7 copy-start.5
  185.5 0.6 copy-start.4
  185.5 0.6 copy-start.6
  189.5 2.7 copy-start.3
  189.5 2.7 copy-start.5
  192.2 0.6 copy-start.4
  192.2 0.6 copy-start.6
  196.2 2.7 copy-start.3
  196.2 2.7 copy-start.5
  198.9 0.6 copy-start.4
  198.9 0.6 copy-start.6
  202.8 2.7 copy-start.3
  202.8 2.7 copy-start.5
  205.5 0.6 copy-start.4
  205.6 0.6 copy-start.6
  209.5 2.7 copy-start.3
  209.5 2.7 copy-start.5
  212.2 0.6 copy-start.4
  212.2 0.6 copy-start.6
  216.2 2.7 copy-start.3
  216.2 2.7 copy-start.5
  218.9 0.6 copy-start.4
  218.9 0.6 copy-start.6
  230.1 11.5 %all-to-all-start.3 = ((f32[8,1,768]{2,1,0:T(1,128)}), f32[8,1,768]{2,1,0:T(1,128)}, u32[]{:S(2)}, u32[]{:S(2)}) async-start(f32[8,1,768]{2,1,0:T(1,128)} %reshape.145), calls=%async_computation.4 | async-start | bytes 49152 | tf_op jit(solution)/shard_map/all_to_all | solution.py:120
  241.7 9.6 %all-to-all-start.4 = ((f32[8,1,768]{2,1,0:T(1,128)}), f32[8,1,768]{2,1,0:T(1,128)}, u32[]{:S(2)}, u32[]{:S(2)}) async-start(f32[8,1,768]{2,1,0:T(1,128)} %reshape.143), calls=%async_computation.5 | async-start | bytes 49152 | tf_op jit(solution)/shard_map/all_to_all | solution.py:121
  251.2 42.0 %all-to-all-start.2 = ((f32[1,1024,768]{2,0,1:T(1,128)}), f32[1,1024,768]{2,0,1:T(1,128)S(1)}, u32[]{:S(2)}, u32[]{:S(2)}) async-start(f32[1,1024,768]{2,0,1:T(1,128)} %copy.112), calls=%async_computation.3 | async-start | bytes 6291456 | tf_op jit(solution)/shard_map/all_to_all | solution.py:117
  293.3 1.9 copy-start
  295.2 1.0 copy-start.7
Sparse Core Ops, SparseCore 0:
  10.4 39.7 all-gather.2
  55.4 84.1 reduce-scatter.1
  142.0 29.6 all-gather.4
where the time goes:
time: 305 us; the launch traced here: 303 us
  waiting for transfers between devices  159 us (52%)
  local copies, waits for them, and re-layouts  51.4 us (17%)
  matrix products  30.4 us (10%)
  other arithmetic  23.7 us (8%)
  starting transfers between devices  19.5 us (6%)
  between operations  13.9 us (5%)
  loops' own time  5.28 us (2%)
    reduce_scatter x1, waiting for transfers between devices, body(): lax.psum_scatter(jnp.dot(columns, joined, preferred_element_type=jnp.floa...  84.3 us
    all_gather x1, waiting for transfers between devices, body(): gathered = lax.all_gather(normed, 'stream', axis=0, tiled=True)  39.8 us
    all_to_all x1, waiting for transfers between devices, body(): lax.all_to_all(numer.reshape(1, -1, width), 'patch', split_axis=1, concat...  18.5 us
    dot_general x7, matrix products, fold_block(): jnp.einsum('thd,khd->thk', all_queries, key_rows.reshape(-1, HEADS, HD),...  13.5 us
    all_to_all x1, waiting for transfers between devices, body(): lax.all_to_all(outgoing, 'patch', split_axis=0, concat_axis=0, tiled=True)  13.4 us
    unnamed x23, local copies, waits for them, and re-layouts  13.4 us
    dot_general x7, matrix products, fold_block(): jnp.einsum('thk,khd->thd', weights, value_rows.reshape(-1, HEADS, HD), pr...  10.5 us
    unnamed x2, other arithmetic  7.58 us
  transfers between devices with their start and end apart: 8, of which 5 were waited for; matrix products, arithmetic and copies ran while one was open for 13% of the time, Pallas kernels for 0%

commit v1 on v0

--- a/solution.py
+++ b/solution.py
@@ -1,3 +1,4 @@
+import functools
 import math
 import jax
 import jax.numpy as jnp
@@ -12,6 +13,25 @@
 masked_score = -1e30
 
 
+def _render_shards(local_values, dev_axis):
+    vals = []
+    world = lax.axis_size(dev_axis)
+    tick = 0
+    while tick < world:
+        vals.append((tick, (tick + 1) % world))
+        tick += 1
+    finding = [None] * world
+    finding[world - 1] = local_values
+    for dev_i in range(world - 2, -1, -1):
+        finding[dev_i] = lax.ppermute(finding[dev_i + 1], dev_axis, vals)
+    step_out = jnp.concatenate(finding, axis=0)
+    prior = (lax.axis_index(dev_axis) + 1) * local_values.shape[0]
+    return jnp.roll(step_out, prior, axis=0)
+
+
+columns_group = functools.partial(_render_shards, dev_axis="stream")
+
+
 def body(tokens, query_weight, key_weight, value_weight, cache_keys, cache_values, lengths, assign):
     owners = lax.axis_size("patch")
     span_rows = tokens.shape[1]
@@ -20,7 +40,7 @@
     normed = (
         floats * lax.rsqrt(jnp.mean(floats * floats, axis=-1, keepdims=True) + epsilon)
     ).astype(jnp.bfloat16)
-    gathered = lax.all_gather(normed, "stream", axis=0, tiled=True)
+    gathered = columns_group(normed)
     shard_rows = query_weight.shape[0]
     offset = lax.axis_index("stream") * shard_rows
     columns = lax.dynamic_slice_in_dim(gathered, offset, shard_rows, 1)

time: 305 us -> 300 us (0.984)
  waiting for transfers between devices: 159 us -> 153 us
  starting transfers between devices: 19.5 us -> 22.6 us
    all_gather x1 -> x0, waiting for transfers between devices: 39.8 us -> none  [body(): gathered = lax.all_gather(normed, 'stream', axis=0, tiled=True)]
    ppermute x0 -> x3, waiting for transfers between devices: none -> 34.4 us  [_render_shards(): finding[dev_i] = lax.ppermute(finding[dev_i + 1], dev_axis, vals)]
    ppermute x0 -> x3, starting transfers between devices: none -> 3.11 us  [_render_shards(): finding[dev_i] = lax.ppermute(finding[dev_i + 1], dev_axis, vals)]
    unnamed x23 -> x37, local copies, waits for them, and re-layouts: 13.4 us -> 13.5 us
    unnamed x2 -> x3, other arithmetic: 7.58 us -> 7.71 us
  transfers between devices with their start and end apart: 8 -> 10, of which waited for: 5 -> 7; matrix products, arithmetic and copies ran while one was open for 13% -> 13% of each run, Pallas kernels for 0% -> 0%
where the time goes in v1:
time: 300 us; the launch traced here: 299 us
  waiting for transfers between devices  153 us (51%)
  local copies, waits for them, and re-layouts  51.6 us (17%)
  matrix products  28.9 us (10%)
  other arithmetic  23.3 us (8%)
  starting transfers between devices  22.6 us (8%)
  between operations  14.3 us (5%)
  loops' own time  5.28 us (2%)
    reduce_scatter x1, waiting for transfers between devices, body(): lax.psum_scatter(jnp.dot(columns, joined, preferred_element_type=jnp.floa...  83.2 us
    ppermute x3, waiting for transfers between devices, _render_shards(): finding[dev_i] = lax.ppermute(finding[dev_i + 1], dev_axis, vals)  34.4 us
    all_to_all x1, waiting for transfers between devices, body(): lax.all_to_all(numer.reshape(1, -1, width), 'patch', split_axis=1, concat...  18.5 us
    unnamed x37, local copies, waits for them, and re-layouts  13.5 us
    dot_general x7, matrix products, fold_block(): jnp.einsum('thd,khd->thk', all_queries, key_rows.reshape(-1, HEADS, HD),...  13.5 us
    all_to_all x1, waiting for transfers between devices, body(): lax.all_to_all(outgoing, 'patch', split_axis=0, concat_axis=0, tiled=True)  13.4 us
    dot_general x7, matrix products, fold_block(): jnp.einsum('thk,khd->thd', weights, value_rows.reshape(-1, HEADS, HD), pr...  10.5 us
    unnamed x3, other arithmetic  7.71 us
  transfers between devices with their start and end apart: 10, of which 7 were waited for; matrix products, arithmetic and copies ran while one was open for 13% of the time, Pallas kernels for 0%

profile of v1, /device:TPU:0, one launch (start us, length us, event | category | flops | bytes accessed | tf_op | source)
XLA Modules:
  0.0 298.6 jit_solution(14723156463012924718)
XLA Ops:
  9.6 3.1 %collective-permute-start = (bf16[128,1536]{1,0:T(8,128)(2,1)S(1)}, bf16[128,1536]{1,0:T(8,128)(2,1)S(1)}, u32[]{:S(2)}, u32[]{:S(2)}) collective-permute-start(bf16[128,1536]{1,0:T(8,128)(2,1)S(1)} %fusion.17), channel_id=1, source_target_pairs={{0,8},{8,16},{16,24},{24,0},{1,9},{9,17},{17,25},{25,1},{2,10},{10... | collective-permute-start | bytes 1179656 | tf_op jit(solution)/shard_map/ppermute | solution.py:26
  12.7 11.1 %collective-permute-done = bf16[128,1536]{1,0:T(8,128)(2,1)S(1)} collective-permute-done((bf16[128,1536]{1,0:T(8,128)(2,1)S(1)}, bf16[128,1536]{1,0:T(8,128)(2,1)S(1)}, u32[]{:S(2)}, u32[]{:S(2)}) %collective-permute-start) | collective-permute-done | bytes 393248 | tf_op jit(solution)/shard_map/ppermute | solution.py:26
  23.8 12.1 %collective-permute-done.1 = bf16[128,1536]{1,0:T(8,128)(2,1)S(1)} collective-permute-done((bf16[128,1536]{1,0:T(8,128)(2,1)S(1)}, bf16[128,1536]{1,0:T(8,128)(2,1)S(1)}, u32[]{:S(2)}, u32[]{:S(2)}) %collective-permute-start.1) | collective-permute-done | bytes 393248 | tf_op jit(solution)/shard_map/ppermute | solution.py:26
  35.9 11.2 %collective-permute-done.2 = bf16[128,1536]{1,0:T(8,128)(2,1)S(1)} collective-permute-done((bf16[128,1536]{1,0:T(8,128)(2,1)S(1)}, bf16[128,1536]{1,0:T(8,128)(2,1)S(1)}, u32[]{:S(2)}, u32[]{:S(2)}) %collective-permute-start.2) | collective-permute-done | bytes 393248 | tf_op jit(solution)/shard_map/ppermute | solution.py:26
  47.6 3.6 %fusion.10 = f32[512,2304]{1,0:T(8,128)} fusion(bf16[384,768]{1,0:T(8,128)(2,1)S(1)} %copy-done.11, bf16[384,768]{1,0:T(8,128)(2,1)S(1)} %copy-done.12, bf16[384,768]{1,0:T(8,128)(2,1)S(1)} %copy-done.13, bf16[1024,1536]{1,0:T(8,128)(2,1)S(1)} %constant_dynamic-update-slice_fusion, s32[]{:T(128)S(6)} %select_n.36, s32[]{:T(128)S(6)} %select_n.38), kind=kOutput, calls=%fused_computation.25 | convolution fusion | flops 911278080 | bytes 6881288 | tf_op jit(solution)/shard_map/dot_general | solution.py:49
  51.3 83.2 %reduce-scatter.2.cloned.1.call-done = f32[128,2304]{1,0:T(8,128)} async-done(((f32[512,2304]{1,0:T(8,128)}), f32[128,2304]{1,0:T(8,128)}) %reduce-scatter.2.cloned.1.call-update) | async-done | bytes 1179664 | tf_op jit(solution)/shard_map/reduce_scatter | solution.py:48
  137.5 3.7 %all-to-all-start = ((bf16[8,8,1]{1,2,0:T(2,128)(2,1)}), bf16[8,8,1]{1,2,0:T(2,128)(2,1)S(1)}, u32[]{:S(2)}, u32[]{:S(2)}) async-start(bf16[8,8,1]{1,2,0:T(2,128)(2,1)} %all_to_all.52), calls=%async_computation | async-start | bytes 8192 | tf_op jit(solution)/shard_map/all_to_all | solution.py:78
  141.5 1.4 fusion.5
  142.8 3.0 all-to-all-done
  145.8 3.5 %all-to-all-start.1 = ((bf16[8,8,6144]{2,1,0:T(8,128)(2,1)}), bf16[8,8,6144]{2,1,0:T(8,128)(2,1)S(1)}, u32[]{:S(2)}, u32[]{:S(2)}) async-start(bf16[8,8,6144]{2,1,0:T(8,128)(2,1)} %fusion.5), calls=%async_computation.2 | async-start | bytes 1572864 | tf_op jit(solution)/shard_map/all_to_all | solution.py:77
  149.4 1.5 copy.109
  150.8 1.4 copy.110
  152.6 13.4 %all-to-all-done.1 = bf16[8,8,6144]{2,1,0:T(8,128)(2,1)S(1)} async-done(((bf16[8,8,6144]{2,1,0:T(8,128)(2,1)}), bf16[8,8,6144]{2,1,0:T(8,128)(2,1)S(1)}, u32[]{:S(2)}, u32[]{:S(2)}) %all-to-all-start.1) | async-done | bytes 786464 | tf_op jit(solution)/shard_map/all_to_all | solution.py:77
  167.9 1.7 copy.104
  169.6 1.6 copy.111
  172.4 2.1 convert_reduce_fusion.1
  176.0 40.9 %while.14 = (s32[]{:T(128)}, f32[1024,6]{0,1:T(8,128)}, f32[1024,6,128]{0,2,1:T(8,128)S(1)}, f32[1024,6]{0,1:T(8,128)}, s32[]{:T(128)}, /*index=5*/bf16[768,768]...) while((s32[]{:T(128)}, f32[1024,6]{0,1:T(8,128)}, ...), condition=%wide.region_9.10_spmd, body=%wide.region_6.9_spmd.sunk | while | flops 412901376 | bytes 19218712 | solution.py:135
  177.7 2.1 bitcast_reduce_fusion.3
  181.0 1.6 fusion.49
  184.4 2.1 bitcast_reduce_fusion.3
  187.7 1.6 fusion.49
  191.1 2.1 bitcast_reduce_fusion.3
  194.4 1.6 fusion.49
  197.8 2.1 bitcast_reduce_fusion.3
  201.1 1.6 fusion.49
  204.4 2.1 bitcast_reduce_fusion.3
  207.7 1.6 fusion.49
  211.1 2.1 bitcast_reduce_fusion.3
  214.4 1.6 fusion.49
  216.9 1.8 copy.113
  219.2 3.8 %reduce.6 = f32[1024,6]{1,0:T(8,128)} reduce(f32[1024,1,6]{2,1,0:T(1,128)} %bitcast.98, f32[]{:T(128)} %broadcast.74), dimensions={1}, to_apply=%bitcast.56.reduce_sub_computation | reduce | bytes 49156
  223.0 2.0 reshape.145
  225.0 3.9 %all-to-all-start.3 = ((f32[8,1,768]{2,1,0:T(1,128)}), f32[8,1,768]{2,1,0:T(1,128)}, u32[]{:S(2)}, u32[]{:S(2)}) async-start(f32[8,1,768]{2,1,0:T(1,128)} %reshape.145), calls=%async_computation.4 | async-start | bytes 49152 | tf_op jit(solution)/shard_map/all_to_all | solution.py:140
  229.0 1.8 copy.117
  230.7 3.8 %reduce.4 = f32[1024,6]{1,0:T(8,128)} reduce(f32[1024,1,6]{2,1,0:T(1,128)} %bitcast.99, f32[]{:T(128)} %broadcast.74), dimensions={1}, to_apply=%bitcast.54.reduce_sub_computation | reduce | bytes 49156
  234.5 2.0 reshape.143
  236.6 4.1 %all-to-all-start.4 = ((f32[8,1,768]{2,1,0:T(1,128)}), f32[8,1,768]{2,1,0:T(1,128)}, u32[]{:S(2)}, u32[]{:S(2)}) async-start(f32[8,1,768]{2,1,0:T(1,128)} %reshape.143), calls=%async_computation.5 | async-start | bytes 49152 | tf_op jit(solution)/shard_map/all_to_all | solution.py:141
  240.7 5.5 %copy.112 = f32[1,1024,768]{2,0,1:T(1,128)} copy(f32[1,1024,768]{1,2,0:T(8,128)S(1)} %bitcast.86) | data formatting | bytes 6291456 | tf_op jit(solution)/shard_map/reshape | solution.py:138
  246.1 4.2 %all-to-all-start.2 = ((f32[1,1024,768]{2,0,1:T(1,128)}), f32[1,1024,768]{2,0,1:T(1,128)S(1)}, u32[]{:S(2)}, u32[]{:S(2)}) async-start(f32[1,1024,768]{2,0,1:T(1,128)} %copy.112), calls=%async_computation.3 | async-start | bytes 6291456 | tf_op jit(solution)/shard_map/all_to_all | solution.py:137
  250.3 2.0 broadcast_in_dim_reshape.6
  253.3 1.4 reduce.7
  254.7 1.7 reshape.146
  258.8 1.5 reduce.5
  260.2 1.7 reshape.144
  263.2 1.9 mul.121
  265.1 3.6 %copy.116 = f32[1,8,128,768]{3,2,1,0:T(8,128)} copy(f32[1,8,128,768]{2,3,1,0:T(8,128)} %bitcast.92) | data formatting | bytes 6291456 | tf_op jit(solution)/shard_map/mul | solution.py:146
  269.6 18.5 %all-to-all-done.2 = f32[1,1024,768]{2,0,1:T(1,128)S(1)} async-done(((f32[1,1024,768]{2,0,1:T(1,128)}), f32[1,1024,768]{2,0,1:T(1,128)S(1)}, u32[]{:S(2)}, u32[]{:S(2)}) %all-to-all-start.2) | async-done | bytes 3145760 | tf_op jit(solution)/shard_map/all_to_all | solution.py:137
  288.4 1.7 copy-done
  (138 shorter events, 32.8 us)
Async XLA Ops:
  7.2 40.1 %copy-start.1 = (bf16[1,128,1536]{2,1,0:T(8,128)(2,1)S(1)}, bf16[1,128,1536]{2,1,0:T(8,128)(2,1)}, u32[]{:S(2)}) copy-start(bf16[1,128,1536]{2,1,0:T(8,128)(2,1)} %param.10) | copy-start | bytes 1179652
  7.2 127.3 %reduce-scatter.2.cloned.1.call-start = ((), (), s32[]{:S(2)}) async-start(), calls=%async_computation.6 | async-start | bytes 5898240 | tf_op jit(solution)/shard_map/reduce_scatter | solution.py:48
  9.6 14.2 %collective-permute-start = (bf16[128,1536]{1,0:T(8,128)(2,1)S(1)}, bf16[128,1536]{1,0:T(8,128)(2,1)S(1)}, u32[]{:S(2)}, u32[]{:S(2)}) collective-permute-start(bf16[128,1536]{1,0:T(8,128)(2,1)S(1)} %fusion.17), channel_id=1, source_target_pairs={{0,8},{8,16},{16,24},{24,0},{1,9},{9,17},{17,25},{25,1},{2,10},{10... | collective-permute-start | bytes 1179656 | tf_op jit(solution)/shard_map/ppermute | solution.py:26
  23.8 12.1 %collective-permute-start.1 = (bf16[128,1536]{1,0:T(8,128)(2,1)S(1)}, bf16[128,1536]{1,0:T(8,128)(2,1)S(1)}, u32[]{:S(2)}, u32[]{:S(2)}) collective-permute-start(bf16[128,1536]{1,0:T(8,128)(2,1)S(1)} %collective-permute-done), channel_id=1, source_target_pairs={{0,8},{8,16},{16,24},{24,0},{1,9},{9,17},{17,25},{25,1},{2,10},{10... | collective-permute-start | bytes 1179656 | tf_op jit(solution)/shard_map/ppermute | solution.py:26
  35.9 11.2 %collective-permute-start.2 = (bf16[128,1536]{1,0:T(8,128)(2,1)S(1)}, bf16[128,1536]{1,0:T(8,128)(2,1)S(1)}, u32[]{:S(2)}, u32[]{:S(2)}) collective-permute-start(bf16[128,1536]{1,0:T(8,128)(2,1)S(1)} %collective-permute-done.1), channel_id=1, source_target_pairs={{0,8},{8,16},{16,24},{24,0},{1,9},{9,17},{17,25},{25,1},{2,10},{10... | collective-permute-start | bytes 1179656 | tf_op jit(solution)/shard_map/ppermute | solution.py:26
  35.9 11.7 %copy-start.11 = (bf16[384,768]{1,0:T(8,128)(2,1)S(1)}, bf16[384,768]{1,0:T(8,128)(2,1)}, u32[]{:S(2)}) copy-start(bf16[384,768]{1,0:T(8,128)(2,1)} %param.13) | copy-start | bytes 1769476
  35.9 11.7 %copy-start.12 = (bf16[384,768]{1,0:T(8,128)(2,1)S(1)}, bf16[384,768]{1,0:T(8,128)(2,1)}, u32[]{:S(2)}) copy-start(bf16[384,768]{1,0:T(8,128)(2,1)} %param.12) | copy-start | bytes 1769476
  35.9 11.7 %copy-start.13 = (bf16[384,768]{1,0:T(8,128)(2,1)S(1)}, bf16[384,768]{1,0:T(8,128)(2,1)}, u32[]{:S(2)}) copy-start(bf16[384,768]{1,0:T(8,128)(2,1)} %param.11) | copy-start | bytes 1769476
  51.2 85.3 %copy-start.14 = (s32[1,32,1]{1,2,0:T(1,128)S(1)}, s32[1,32,1]{1,2,0:T(1,128)}, u32[]{:S(2)}) copy-start(s32[1,32,1]{1,2,0:T(1,128)} %param.17) | copy-start | bytes 388
  51.3 98.1 %copy-start.9 = (bf16[1,768,768]{2,1,0:T(8,128)(2,1)S(1)}, bf16[1,768,768]{2,1,0:T(8,128)(2,1)}, u32[]{:S(2)}) copy-start(bf16[1,768,768]{2,1,0:T(8,128)(2,1)} %param.14) | copy-start | bytes 3538948
  51.3 116.6 %all-gather.2.cloned.1.call-start = ((), (), s32[]{:S(2)}) async-start(), calls=%async_computation.7 | async-start | bytes 1769472 | tf_op jit(solution)/shard_map/all_gather | solution.py:84
  136.5 14.3 %copy-start.10 = (bf16[1,768,768]{2,1,0:T(8,128)(2,1)S(1)}, bf16[1,768,768]{2,1,0:T(8,128)(2,1)}, u32[]{:S(2)}) copy-start(bf16[1,768,768]{2,1,0:T(8,128)(2,1)} %param.15) | copy-start | bytes 3538948
  137.5 8.3 %all-to-all-start = ((bf16[8,8,1]{1,2,0:T(2,128)(2,1)}), bf16[8,8,1]{1,2,0:T(2,128)(2,1)S(1)}, u32[]{:S(2)}, u32[]{:S(2)}) async-start(bf16[8,8,1]{1,2,0:T(2,128)(2,1)} %all_to_all.52), calls=%async_computation | async-start | bytes 8192 | tf_op jit(solution)/shard_map/all_to_all | solution.py:78
  145.8 20.2 %all-to-all-start.1 = ((bf16[8,8,6144]{2,1,0:T(8,128)(2,1)}), bf16[8,8,6144]{2,1,0:T(8,128)(2,1)S(1)}, u32[]{:S(2)}, u32[]{:S(2)}) async-start(bf16[8,8,6144]{2,1,0:T(8,128)(2,1)} %fusion.5), calls=%async_computation.2 | async-start | bytes 1572864 | tf_op jit(solution)/shard_map/all_to_all | solution.py:77
  166.1 1.8 copy-start.2
  172.4 2.7 copy-start.3
  177.7 2.7 copy-start.4
  177.7 2.7 copy-start.6
  180.4 0.6 copy-start.5
  180.4 0.6 copy-start.7
  184.4 2.7 copy-start.4
  184.4 2.7 copy-start.6
  187.1 0.6 copy-start.5
  187.1 0.6 copy-start.7
  191.1 2.7 copy-start.4
  191.1 2.7 copy-start.6
  193.8 0.6 copy-start.5
  193.8 0.6 copy-start.7
  197.7 2.7 copy-start.4
  197.7 2.7 copy-start.6
  200.4 0.6 copy-start.5
  200.5 0.6 copy-start.7
  204.4 2.7 copy-start.4
  204.4 2.7 copy-start.6
  207.1 0.6 copy-start.5
  207.1 0.6 copy-start.7
  211.1 2.7 copy-start.4
  211.1 2.7 copy-start.6
  213.8 0.6 copy-start.5
  213.8 0.6 copy-start.7
  225.0 11.5 %all-to-all-start.3 = ((f32[8,1,768]{2,1,0:T(1,128)}), f32[8,1,768]{2,1,0:T(1,128)}, u32[]{:S(2)}, u32[]{:S(2)}) async-start(f32[8,1,768]{2,1,0:T(1,128)} %reshape.145), calls=%async_computation.4 | async-start | bytes 49152 | tf_op jit(solution)/shard_map/all_to_all | solution.py:140
  236.6 9.6 %all-to-all-start.4 = ((f32[8,1,768]{2,1,0:T(1,128)}), f32[8,1,768]{2,1,0:T(1,128)}, u32[]{:S(2)}, u32[]{:S(2)}) async-start(f32[8,1,768]{2,1,0:T(1,128)} %reshape.143), calls=%async_computation.5 | async-start | bytes 49152 | tf_op jit(solution)/shard_map/all_to_all | solution.py:141
  246.1 42.0 %all-to-all-start.2 = ((f32[1,1024,768]{2,0,1:T(1,128)}), f32[1,1024,768]{2,0,1:T(1,128)S(1)}, u32[]{:S(2)}, u32[]{:S(2)}) async-start(f32[1,1024,768]{2,0,1:T(1,128)} %copy.112), calls=%async_computation.3 | async-start | bytes 6291456 | tf_op jit(solution)/shard_map/all_to_all | solution.py:137
  288.2 1.9 copy-start
  290.1 1.0 copy-start.8
Sparse Core Ops, SparseCore 0:
  51.4 83.0 reduce-scatter.1
  136.9 29.6 all-gather.1
